TPU v7x, 32 devices: a whole 2x2x4 slice. The times are simulated.
32 devices in a mesh: zero: 8 (over y, x, core), cols: 4 (over z).
Axes of the slice: x: 2, y: 2, z: 4, core: 2. Of those that a mesh axis runs over, the one named last changes fastest.
Arguments:
- train_gate: bfloat16 [4096, 11008], P('zero', 'cols'), may hold values from -0.125 to 0.125
- low_gate: bfloat16 [4096, 64], P('zero'), may hold values from -0.09375 to 0.09375
- high_gate: bfloat16 [64, 11008], P(None, 'cols'), may hold values from -0.75 to 0.75
- train_up: bfloat16 [4096, 11008], P('zero', 'cols'), may hold values from -0.125 to 0.125
- low_up: bfloat16 [4096, 64], P('zero'), may hold values from -0.09375 to 0.09375
- high_up: bfloat16 [64, 11008], P(None, 'cols'), may hold values from -0.75 to 0.75
- norm_train: float32 [4096], P(('zero', 'cols')), may hold values from 0.25 to 1.75
- norm_step: float32 [4096], P(('zero', 'cols')), may hold values from -0.3 to 0.3
Outputs:
- ready_gate: bfloat16 [4096, 11008], P(None, 'cols')
- ready_up: bfloat16 [4096, 11008], P(None, 'cols')
- factor_gate: float32 [11008], P('cols')
- factor_up: float32 [11008], P('cols')
- serve_norm: bfloat16 [4096], replicated
All inputs are finite; a program needn't handle non-finite values. Where the computation divides by a largest or mean magnitude, that divisor is 1e-20 or more.
Results may differ from a plain program's by a relative error of at most 0.001.
Values may be sent and summed in bfloat16 or wider, within the bound.
A program may use at most 192 MiB of HBM per device.

v0:
```python
import jax
import jax.numpy as jnp
from jax import lax
from jax.sharding import PartitionSpec as P

D_MODEL = 4096
mix_rate = 1.0


def shards(train_gate, low_gate, high_gate, train_up, low_up, high_up, norm_train, norm_step):
    latest_gate = train_gate.astype(jnp.float32) + mix_rate * jnp.dot(
        low_gate, high_gate, preferred_element_type=jnp.float32
    )
    latest_up = train_up.astype(jnp.float32) + mix_rate * jnp.dot(
        low_up, high_up, preferred_element_type=jnp.float32
    )
    total_gate, total_up = lax.psum(
        (jnp.sum(jnp.abs(latest_gate), axis=0), jnp.sum(jnp.abs(latest_up), axis=0)), "zero"
    )
    factor_gate = total_gate / D_MODEL
    factor_up = total_up / D_MODEL
    narrow_gate, narrow_up = (
        (latest_gate / factor_gate).astype(jnp.bfloat16),
        (latest_up / factor_up).astype(jnp.bfloat16),
    )
    ready_gate, ready_up = (
        lax.all_gather(narrow_gate, "zero", axis=0, tiled=True),
        lax.all_gather(narrow_up, "zero", axis=0, tiled=True),
    )
    serve_norm = lax.all_gather(
        (norm_train + norm_step).astype(jnp.bfloat16), ("zero", "cols"), axis=0, tiled=True
    )
    return (ready_gate, ready_up, factor_gate, factor_up, serve_norm)


def solution(mesh):
    return jax.shard_map(
        shards,
        mesh=mesh,
        in_specs=(
            P("zero", "cols"),
            P("zero", None),
            P(None, "cols"),
            P("zero", "cols"),
            P("zero", None),
            P(None, "cols"),
            P(("zero", "cols")),
            P(("zero", "cols")),
        ),
        out_specs=(P(None, "cols"), P(None, "cols"), P("cols"), P("cols"), P()),
        check_vma=False,
    )
```

profile of v0, /device:TPU:0, one launch (start us, length us, event | category | flops | bytes accessed | tf_op | source)
XLA Modules:
  0.0 323.6 jit_solution(7522673026313851749)
XLA Ops:
  7.2 0.0 copy-start
  7.2 0.0 copy-start.3
  7.2 0.0 copy-start.4
  7.2 0.0 all-gather.6.cloned.1.call-start
  7.2 0.9 copy-done
  8.2 0.0 copy-start.5
  8.2 5.4 %abs_reduce_fusion.1 = (f32[2752]{0:T(1024)S(1)}, f32[512,2752]{0,1:T(8,128)}) fusion(bf16[512,64]{0,1:T(8,128)(2,1)} %param.9, bf16[64,2752]{1,0:T(8,128)(2,1)S(1)} %copy-done, bf16[512,2752]{0,1:T(8,128)(2,1)} %param.8), kind=kOutput, calls=%fused_computation.4 | convolution fusion | flops 185988416 | bytes 8882944 | tf_op jit(solution)/shard_map/dot_general | solution.py:11
  13.6 0.0 copy-done.3
  13.6 0.0 copy-done.4
  13.6 0.0 copy-done.5
  13.6 3.5 %abs_reduce_fusion = (f32[2752]{0:T(1024)S(1)}, f32[512,2752]{0,1:T(8,128)}) fusion(bf16[512,64]{0,1:T(8,128)(2,1)S(1)} %copy-done.5, bf16[64,2752]{1,0:T(8,128)(2,1)S(1)} %copy-done.4, bf16[512,2752]{0,1:T(8,128)(2,1)S(1)} %copy-done.3), kind=kOutput, calls=%fused_computation.1 | convolution fusion | flops 185988416 | bytes 8882944 | tf_op jit(solution)/shard_map/dot_general | solution.py:14
  17.2 25.5 %all-reduce = (f32[2752]{0:T(1024)S(1)}, f32[2752]{0:T(1024)S(1)}) all-reduce(f32[2752]{0:T(1024)S(1)} %get-tuple-element.7, f32[2752]{0:T(1024)S(1)} %get-tuple-element.9), channel_id=1, replica_groups=mesh['zero'=8,'cols'=4] {'zero'}, use_global_device_ids=true, to_apply=%region_1.0 | all-reduce | flops 5504 | bytes 44032 | tf_op jit(solution)/shard_map/psum | solution.py:17
  42.7 0.0 copy-start.6
  42.7 4.4 %divide_convert_fusion = bf16[512,2752]{0,1:T(8,128)(2,1)} fusion(f32[512,2752]{0,1:T(8,128)} %get-tuple-element.10, f32[2752]{0:T(1024)S(1)} %broadcast_multiply_fusion), kind=kLoop, calls=%fused_computation | loop fusion | flops 2818048 | bytes 8465152 | tf_op jit(solution)/shard_map/convert_element_type | solution.py:24
  47.1 0.0 all-gather.6.cloned.1.call-update
  47.2 0.0 copy-done.6
  47.2 0.0 all-gather.4.cloned.1.call-start
  47.2 0.0 copy-start.7
  47.2 0.0 copy-start.8
  47.2 0.0 copy-start.9
  47.3 4.4 %divide_convert_fusion.1 = bf16[512,2752]{0,1:T(8,128)(2,1)} fusion(f32[512,2752]{0,1:T(8,128)} %get-tuple-element.8, f32[2752]{0:T(1024)S(1)} %broadcast_multiply_fusion.1), kind=kLoop, calls=%fused_computation.3 | loop fusion | flops 2818048 | bytes 8465152 | tf_op jit(solution)/shard_map/convert_element_type | solution.py:23
  51.6 0.0 all-gather.4.cloned.1.call-update
  51.7 0.0 copy-done.7
  51.7 0.0 copy-done.8
  51.7 0.0 copy-done.9
  51.7 66.0 %all-gather = bf16[32,1,128]{2,1,0:T(2,128)(2,1)S(1)} all-gather(bf16[1,1,128]{2,1,0:T(2,128)(2,1)S(1)} %convert_bitcast_fusion), channel_id=1, replica_groups=mesh['zero'=8,'cols'=4] {'zero','cols'}, dimensions={0}, use_global_device_ids=true | all-gather | bytes 8448 | tf_op jit(solution)/shard_map/all_gather | solution.py:30
  117.7 0.6 reduce
  118.3 47.0 %all-gather.6.cloned.1.call-done = bf16[4096,2752]{0,1:T(8,128)(2,1)} async-done(((bf16[512,2752]{0,1:T(8,128)(2,1)}), bf16[4096,2752]{0,1:T(8,128)(2,1)}) %all-gather.6.cloned.1.call-update) | async-done | bytes 22544400 | tf_op jit(solution)/shard_map/all_gather | solution.py:28
  165.3 121.0 %all-gather.4.cloned.1.call-done = bf16[4096,2752]{0,1:T(8,128)(2,1)} async-done(((bf16[512,2752]{0,1:T(8,128)(2,1)}), bf16[4096,2752]{0,1:T(8,128)(2,1)}) %all-gather.4.cloned.1.call-update) | async-done | bytes 22544400 | tf_op jit(solution)/shard_map/all_gather | solution.py:27
  286.3 0.0 copy-start.2
  286.4 21.1 %copy.15 = bf16[4096,2752]{0,1:T(8,128)(2,1)} copy(bf16[4096,2752]{0,1:T(8,128)(2,1)} %all-gather.4.cloned.1.call-done) | data formatting | bytes 45088768
  307.5 1.2 copy-done.2
  308.7 0.0 copy-start.1
  308.7 8.1 %copy.16 = bf16[4096,2752]{0,1:T(8,128)(2,1)} copy(bf16[4096,2752]{0,1:T(8,128)(2,1)S(1)} %copy-done.2) | data formatting | bytes 45088768
  316.7 0.0 copy-done.1
  (3 shorter events, 0.0 us)
Async XLA Ops:
  7.2 1.0 copy-start
  7.2 6.4 %copy-start.3 = (bf16[512,2752]{0,1:T(8,128)(2,1)S(1)}, bf16[512,2752]{0,1:T(8,128)(2,1)}, u32[]{:S(2)}) copy-start(bf16[512,2752]{0,1:T(8,128)(2,1)} %param.11) | copy-start | bytes 8454148
  7.2 6.4 %copy-start.4 = (bf16[64,2752]{1,0:T(8,128)(2,1)S(1)}, bf16[64,2752]{1,0:T(8,128)(2,1)}, u32[]{:S(2)}) copy-start(bf16[64,2752]{1,0:T(8,128)(2,1)} %param.13) | copy-start | bytes 1056772
  7.2 158.1 %all-gather.6.cloned.1.call-start = ((), (), s32[]{:S(2)}) async-start(), calls=%async_computation.1 | async-start | bytes 25362432 | tf_op jit(solution)/shard_map/all_gather | solution.py:28
  8.2 5.5 %copy-start.5 = (bf16[512,64]{0,1:T(8,128)(2,1)S(1)}, bf16[512,64]{0,1:T(8,128)(2,1)}, u32[]{:S(2)}) copy-start(bf16[512,64]{0,1:T(8,128)(2,1)} %param.12) | copy-start | bytes 196612
  42.7 4.4 %copy-start.6 = (f32[2752]{0:T(1024)}, f32[2752]{0:T(1024)S(1)}, u32[]{:S(2)}) copy-start(f32[2752]{0:T(1024)S(1)} %broadcast_multiply_fusion) | copy-start | bytes 33028
  47.2 239.2 %all-gather.4.cloned.1.call-start = ((), (), s32[]{:S(2)}) async-start(), calls=%async_computation | async-start | bytes 25362432 | tf_op jit(solution)/shard_map/all_gather | solution.py:27
  47.2 4.4 %copy-start.7 = (f32[2752]{0:T(1024)}, f32[2752]{0:T(1024)S(1)}, u32[]{:S(2)}) copy-start(f32[2752]{0:T(1024)S(1)} %broadcast_multiply_fusion.1) | copy-start | bytes 33028
  47.2 4.4 %copy-start.8 = (f32[128]{0:T(128)S(1)}, f32[128]{0:T(128)}, u32[]{:S(2)}) copy-start(f32[128]{0:T(128)} %param.14) | copy-start | bytes 1540
  47.2 4.4 %copy-start.9 = (f32[128]{0:T(128)S(1)}, f32[128]{0:T(128)}, u32[]{:S(2)}) copy-start(f32[128]{0:T(128)} %param.15) | copy-start | bytes 1540
  286.3 22.3 %copy-start.2 = (bf16[4096,2752]{0,1:T(8,128)(2,1)S(1)}, bf16[4096,2752]{0,1:T(8,128)(2,1)}, u32[]{:S(2)}) copy-start(bf16[4096,2752]{0,1:T(8,128)(2,1)} %all-gather.6.cloned.1.call-done) | copy-start | bytes 67633152
  308.7 8.1 %copy-start.1 = (bf16[64,2752]{1,0:T(8,128)(2,1)S(1)}, bf16[64,2752]{1,0:T(8,128)(2,1)}, u32[]{:S(2)}) copy-start(bf16[64,2752]{1,0:T(8,128)(2,1)} %param.10) | copy-start | bytes 1056772
Sparse Core Ops, SparseCore 0:
  47.3 117.9 all-gather.5
  167.8 118.5 all-gather.3
where the time goes:
time: 324 us
  waiting for transfers between devices  168 us (52%)
  blocking collectives  91.5 us (28%)
  local copies, waits for them, and re-layouts  31.3 us (10%)
  between operations  14.1 us (4%)
  other arithmetic  9.46 us (3%)
  matrix products  8.98 us (3%)
    all_gather x1, waiting for transfers between devices, shards(): lax.all_gather(narrow_gate, 'zero', axis=0, tiled=True)  121 us
    all_gather x1, blocking collectives, shards(): lax.all_gather((norm_train + norm_step).astype(jnp.bfloat16), ('zero', 'c...  66 us
    all_gather x1, waiting for transfers between devices, shards(): lax.all_gather(narrow_up, 'zero', axis=0, tiled=True)  47 us
    unnamed x22, local copies, waits for them, and re-layouts  31.3 us
    psum x1, blocking collectives, shards(): lax.psum((jnp.sum(jnp.abs(latest_gate), axis=0), jnp.sum(jnp.abs(latest_u...  25.5 us
  transfers between devices with their start and end apart: 2, of which 2 were waited for; matrix products, arithmetic and copies ran while one was open for 2% of the time, Pallas kernels for 0%

commit v1 on v0

--- a/solution.py
+++ b/solution.py
@@ -25,7 +25,9 @@
     )
     ready_gate, ready_up = (
         lax.all_gather(narrow_gate, "zero", axis=0, tiled=True),
-        lax.all_gather(narrow_up, "zero", axis=0, tiled=True),
+        jnp.concatenate(
+            lax.all_to_all(jnp.stack([narrow_up] * lax.axis_size("zero")), "zero", 0, 0), axis=0
+        ),
     )
     serve_norm = lax.all_gather(
         (norm_train + norm_step).astype(jnp.bfloat16), ("zero", "cols"), axis=0, tiled=True

time: 324 us -> 479 us (1.48)
  waiting for transfers between devices: 168 us -> 256 us
  local copies, waits for them, and re-layouts: 31.3 us -> 88.1 us
  starting transfers between devices: 0.08 us -> 6.56 us
    all_to_all x0 -> x1, waiting for transfers between devices: none -> 256 us  [shards(): lax.all_to_all(jnp.stack([narrow_up] * lax.axis_size('zero')), 'zero', 0, 0)]
    all_gather x1, waiting for transfers between devices: 121 us -> 0.01 us  [shards(): lax.all_gather(narrow_gate, 'zero', axis=0, tiled=True)]
    all_gather x1 -> x0, waiting for transfers between devices: 47 us -> none  [shards(): lax.all_gather(narrow_up, 'zero', axis=0, tiled=True)]
    all_to_all x0 -> x1, local copies, waits for them, and re-layouts: none -> 29.7 us  [shards(): lax.all_to_all(jnp.stack([narrow_up] * lax.axis_size('zero')), 'zero', 0, 0)]
    unnamed x22 -> x20, local copies, waits for them, and re-layouts: 31.3 us -> 49 us
    another operation x0 -> x1, local copies, waits for them, and re-layouts: none -> 9.41 us  [shards(): jnp.stack([narrow_up] * lax.axis_size('zero'))]
    all_to_all x0 -> x1, starting transfers between devices: none -> 6.52 us  [shards(): lax.all_to_all(jnp.stack([narrow_up] * lax.axis_size('zero')), 'zero', 0, 0)]
  transfers between devices with their start and end apart: 2 -> 2, of which waited for: 2 -> 1; matrix products, arithmetic and copies ran while one was open for 2% -> 15% of each run, Pallas kernels for 0% -> 0%
where the time goes in v1:
time: 479 us; the launch traced here: 477 us
  waiting for transfers between devices  256 us (53%)
  blocking collectives  94.6 us (20%)
  local copies, waits for them, and re-layouts  88.1 us (18%)
  between operations  14.1 us (3%)
  matrix products  8.98 us (2%)
  other arithmetic  8.33 us (2%)
  starting transfers between devices  6.56 us (1%)
    all_to_all x1, waiting for transfers between devices, shards(): lax.all_to_all(jnp.stack([narrow_up] * lax.axis_size('zero')), 'zero', 0, 0)  256 us
    all_gather x1, blocking collectives, shards(): lax.all_gather((norm_train + norm_step).astype(jnp.bfloat16), ('zero', 'c...  69 us
    unnamed x20, local copies, waits for them, and re-layouts  49 us
    all_to_all x1, local copies, waits for them, and re-layouts, shards(): lax.all_to_all(jnp.stack([narrow_up] * lax.axis_size('zero')), 'zero', 0, 0)  29.7 us
    psum x1, blocking collectives, shards(): lax.psum((jnp.sum(jnp.abs(latest_gate), axis=0), jnp.sum(jnp.abs(latest_u...  25.5 us
  transfers between devices with their start and end apart: 2, of which 1 were waited for; matrix products, arithmetic and copies ran while one was open for 15% of the time, Pallas kernels for 0%

profile of v1, /device:TPU:0, one launch (start us, length us, event | category | flops | bytes accessed | tf_op | source)
XLA Modules:
  0.0 477.0 jit_solution(14344163282903571455)
XLA Ops:
  7.2 0.0 copy-start
  7.2 0.0 copy-start.2
  7.2 0.0 copy-start.3
  7.2 0.0 all-gather.3.cloned.1.call-start
  7.2 0.9 copy-done
  8.2 0.0 copy-start.4
  8.2 5.4 %abs_reduce_fusion.1 = (f32[2752]{0:T(1024)S(1)}, f32[512,2752]{0,1:T(8,128)}) fusion(bf16[512,64]{0,1:T(8,128)(2,1)} %param.9, bf16[64,2752]{1,0:T(8,128)(2,1)S(1)} %copy-done, bf16[512,2752]{0,1:T(8,128)(2,1)} %param.8), kind=kOutput, calls=%fused_computation.4 | convolution fusion | flops 185988416 | bytes 8882944 | tf_op jit(solution)/shard_map/dot_general | solution.py:11
  13.6 0.0 copy-done.2
  13.6 0.0 copy-done.3
  13.6 0.0 copy-done.4
  13.6 3.5 abs_reduce_fusion
  17.2 25.5 %all-reduce = (f32[2752]{0:T(1024)S(1)}, f32[2752]{0:T(1024)S(1)}) all-reduce(f32[2752]{0:T(1024)S(1)} %get-tuple-element.12, f32[2752]{0:T(1024)S(1)} %get-tuple-element.14), channel_id=1, replica_groups=mesh['zero'=8,'cols'=4] {'zero'}, use_global_device_ids=true, to_apply=%region_1.0 | all-reduce | flops 5504 | bytes 44032 | tf_op jit(solution)/shard_map/psum | solution.py:17
  42.7 0.0 copy-start.5
  42.7 4.4 divide_convert_fusion.1
  47.1 0.0 all-gather.3.cloned.1.call-update
  47.1 0.0 copy-done.5
  47.1 0.0 copy-start.6
  47.2 3.3 divide_convert_fusion
  50.4 9.4 %stack.2 = bf16[8,512,2752]{1,2,0:T(8,128)(2,1)} broadcast(bf16[512,2752]{0,1:T(8,128)(2,1)S(1)} %divide_convert_fusion), dimensions={1,2} | broadcast | bytes 25362432 | tf_op jit(solution)/shard_map/stack | solution.py:29
  59.9 0.0 copy-done.6
  59.9 0.0 copy-start.7
  59.9 0.0 copy-start.8
  59.9 6.5 %all-to-all-start = ((bf16[8,512,2752]{1,2,0:T(8,128)(2,1)}), bf16[8,512,2752]{1,2,0:T(8,128)(2,1)}, u32[]{:S(2)}, u32[]{:S(2)}) async-start(bf16[8,512,2752]{1,2,0:T(8,128)(2,1)} %stack.2), calls=%async_computation | async-start | bytes 45088768 | tf_op jit(solution)/shard_map/all_to_all | solution.py:29
  66.4 0.0 copy-done.7
  66.4 0.0 copy-done.8
  66.4 69.0 %all-gather = bf16[32,1,128]{2,1,0:T(2,128)(2,1)S(1)} all-gather(bf16[1,1,128]{2,1,0:T(2,128)(2,1)S(1)} %convert_bitcast_fusion), channel_id=1, replica_groups=mesh['zero'=8,'cols'=4] {'zero','cols'}, dimensions={0}, use_global_device_ids=true | all-gather | bytes 8448 | tf_op jit(solution)/shard_map/all_gather | solution.py:32
  135.4 0.6 reduce
  136.1 256.4 %all-to-all-done = bf16[8,512,2752]{1,2,0:T(8,128)(2,1)} async-done(((bf16[8,512,2752]{1,2,0:T(8,128)(2,1)}), bf16[8,512,2752]{1,2,0:T(8,128)(2,1)}, u32[]{:S(2)}, u32[]{:S(2)}) %all-to-all-start) | async-done | bytes 22544416 | tf_op jit(solution)/shard_map/all_to_all | solution.py:29
  392.5 29.7 %copy.13 = bf16[8,512,2752]{2,1,0:T(8,128)(2,1)} copy(bf16[8,512,2752]{1,2,0:T(8,128)(2,1)} %all-to-all-done) | data formatting | bytes 45088768 | tf_op jit(solution)/shard_map/all_to_all | solution.py:29
  422.2 28.5 %copy.14 = bf16[4096,2752]{0,1:T(8,128)(2,1)} copy(bf16[4096,2752]{1,0:T(8,128)(2,1)} %bitcast.8) | data formatting | bytes 45088768
  450.7 0.0 all-gather.3.cloned.1.call-done
  450.7 0.0 copy-start.1
  450.7 19.5 %copy.16 = bf16[4096,2752]{0,1:T(8,128)(2,1)} copy(bf16[4096,2752]{0,1:T(8,128)(2,1)} %all-gather.3.cloned.1.call-done) | data formatting | bytes 45088768
  470.2 0.0 copy-done.1
  (3 shorter events, 0.0 us)
Async XLA Ops:
  7.2 1.0 copy-start
  7.2 6.4 %copy-start.2 = (bf16[512,2752]{0,1:T(8,128)(2,1)S(1)}, bf16[512,2752]{0,1:T(8,128)(2,1)}, u32[]{:S(2)}) copy-start(bf16[512,2752]{0,1:T(8,128)(2,1)} %param.11) | copy-start | bytes 8454148
  7.2 6.4 %copy-start.3 = (bf16[64,2752]{1,0:T(8,128)(2,1)S(1)}, bf16[64,2752]{1,0:T(8,128)(2,1)}, u32[]{:S(2)}) copy-start(bf16[64,2752]{1,0:T(8,128)(2,1)} %param.13) | copy-start | bytes 1056772
  7.2 443.5 %all-gather.3.cloned.1.call-start = ((), (), s32[]{:S(2)}) async-start(), calls=%async_computation.1 | async-start | bytes 25362432 | tf_op jit(solution)/shard_map/all_gather | solution.py:27
  8.2 5.5 %copy-start.4 = (bf16[512,64]{0,1:T(8,128)(2,1)S(1)}, bf16[512,64]{0,1:T(8,128)(2,1)}, u32[]{:S(2)}) copy-start(bf16[512,64]{0,1:T(8,128)(2,1)} %param.12) | copy-start | bytes 196612
  42.7 4.4 copy-start.5
  47.1 12.7 %copy-start.6 = (f32[2752]{0:T(1024)}, f32[2752]{0:T(1024)S(1)}, u32[]{:S(2)}) copy-start(f32[2752]{0:T(1024)S(1)} %broadcast_multiply_fusion) | copy-start | bytes 33028
  59.9 6.5 %copy-start.7 = (f32[128]{0:T(128)S(1)}, f32[128]{0:T(128)}, u32[]{:S(2)}) copy-start(f32[128]{0:T(128)} %param.14) | copy-start | bytes 1540
  59.9 6.5 %copy-start.8 = (f32[128]{0:T(128)S(1)}, f32[128]{0:T(128)}, u32[]{:S(2)}) copy-start(f32[128]{0:T(128)} %param.15) | copy-start | bytes 1540
  59.9 332.6 %all-to-all-start = ((bf16[8,512,2752]{1,2,0:T(8,128)(2,1)}), bf16[8,512,2752]{1,2,0:T(8,128)(2,1)}, u32[]{:S(2)}, u32[]{:S(2)}) async-start(bf16[8,512,2752]{1,2,0:T(8,128)(2,1)} %stack.2), calls=%async_computation | async-start | bytes 45088768 | tf_op jit(solution)/shard_map/all_to_all | solution.py:29
  450.7 19.5 %copy-start.1 = (bf16[64,2752]{1,0:T(8,128)(2,1)S(1)}, bf16[64,2752]{1,0:T(8,128)(2,1)}, u32[]{:S(2)}) copy-start(bf16[64,2752]{1,0:T(8,128)(2,1)} %param.10) | copy-start | bytes 1056772
Sparse Core Ops, SparseCore 0:
  47.2 291.6 all-gather.2
